TPU v7x, 32 devices: a whole 2x2x4 slice. The times are simulated.
32 devices in a mesh: row: 4 (over y, core), col: 8 (over z, x).
Axes of the slice: x: 2, y: 2, z: 4, core: 2. Of those that a mesh axis runs over, the one named last changes fastest.
Arguments:
- l_saved: bfloat16 [16, 4, 256, 8, 256], P(None, 'row', None, 'col'), as said below
- l_grad: bfloat16 [16, 4, 256, 8, 256], P(None, 'row', None, 'col'), as said below
Outputs:
- grad_out: float32 [16, 4, 256, 8, 256], P(None, 'row', None, 'col')
Inputs may be any that keep to these rules, and one draw needn't show every extreme that they name: Read as one matrix of 16384 rows, l_saved is lower triangular with its diagonal between 1 and 2. Read as one matrix, l_grad is zero above the diagonal.
All inputs are finite; a program needn't handle non-finite values.
Results may differ from a plain program's by a relative error of at most 0.0003.
Values may be sent and summed in bfloat16 or wider, within the bound.
A program may use at most 64 MiB of HBM per device.

v0:
```python
import jax
import jax.numpy as jnp
from jax import lax
from jax.sharding import PartitionSpec as P

F32 = jnp.float32
BF16 = jnp.bfloat16
HIGH3 = lax.Precision.HIGH


def dot3(a, b, ca=1, cb=0):
    return lax.dot_general(
        a, b, (((ca,), (cb,)), ((), ())), precision=HIGH3, preferred_element_type=F32
    )


def bdot(a, b):
    return lax.dot_general(
        a, b, (((2,), (1,)), ((0,), (0,))), precision=HIGH3, preferred_element_type=F32
    )


def inverse_pair(tiles):
    tile = tiles.shape[-1]
    rows = lax.broadcasted_iota(jnp.int32, (tile, tile), 0)
    cols = lax.broadcasted_iota(jnp.int32, (tile, tile), 1)
    eye = (rows == cols).astype(F32)
    recip = 1.0 / jnp.sum(tiles * eye, axis=2)
    inv = eye * recip[:, None, :]
    size = 1
    while size < tile:
        off = (rows // size % 2 == 1) & (cols // size == rows // size - 1)
        part = jnp.where(off, tiles, 0.0)
        if size == 1:
            inv = inv - recip[:, :, None] * part * recip[:, None, :]
        else:
            inv = inv - bdot(inv, bdot(part, inv))
        size *= 2
    return inv


def per_device(l_saved, l_grad):
    rows_here, tile = (l_saved.shape[0], l_saved.shape[2])
    n_row = lax.axis_size("row")
    n_col = lax.axis_size("col")
    factor = l_saved.reshape(rows_here, tile, tile)
    grad = l_grad.reshape(rows_here, tile, tile)
    my_row = lax.axis_index("row")
    my_col = lax.axis_index("col")
    assert n_col % n_row == 0
    first = n_col // n_row
    loc = first - 1
    lo, hi = (n_col - 2, n_col - 1)
    l_dk = lax.all_gather(factor[loc], "row")[n_row - 2 :].reshape(2 * tile, tile)
    mine = jnp.concatenate([l_dk, grad[first:].reshape(-1, tile)], 0)
    zero = jnp.zeros_like(mine)
    both = jnp.concatenate(
        [jnp.where(my_col == lo, mine, zero), jnp.where(my_col == hi, mine, zero)], 1
    )
    both = lax.psum(both, "col")
    l_dd = both[: 2 * tile].astype(F32)
    g_d = both[2 * tile :]
    l66, l76, l77 = (l_dd[:tile, :tile], l_dd[tile:, :tile], l_dd[tile:, tile:])
    inv = inverse_pair(jnp.stack([l66, l77]))
    w76 = -dot3(inv[1], dot3(l76, inv[0]))
    w = jnp.concatenate(
        [jnp.concatenate([inv[0], jnp.zeros_like(w76)], 1), jnp.concatenate([w76, inv[1]], 1)], 0
    )
    below_l = factor[first:].reshape(-1, tile)
    h = lax.dot_general(g_d, below_l, (((0,), (0,)), ((), ())), preferred_element_type=F32)
    t = dot3(w, lax.psum(h, "row"), 0, 0)
    fresh = grad[loc].astype(F32)
    g_dk = lax.all_gather(grad[loc], "row")[n_row - 2 :].reshape(2 * tile, tile).astype(F32)
    q_mine = g_dk - t
    z2 = jnp.zeros_like(q_mine)
    q = lax.psum(
        jnp.concatenate(
            [jnp.where(my_col == lo, q_mine, z2), jnp.where(my_col == hi, q_mine, z2)], 1
        ),
        "col",
    )
    eye2 = jnp.eye(2 * tile, dtype=F32)
    q = jnp.tril(q)
    m = dot3(l_dd, q, 0, 0)
    phi = jnp.tril(m) - 0.5 * m * eye2
    half = dot3(dot3(w, phi, 0, 0), w)
    s = half + half.T
    out_dd = jnp.tril(s) - 0.5 * s * eye2
    right = my_col >= lo
    w_mine = jnp.where(my_col == lo, w[:, :tile], w[:, tile:])
    x = jnp.where(right, -w_mine, dot3(w, l_dk.astype(F32)))
    x_hi = lax.reduce_precision(x, 8, 7)
    x_lo = (x - x_hi).astype(BF16)
    x_hi = x_hi.astype(BF16)
    prod = jnp.dot(g_d, x_hi, preferred_element_type=F32) + jnp.dot(
        g_d, x_lo, preferred_element_type=F32
    )
    base = jnp.where(right, jnp.zeros((), BF16), grad[first:]).astype(F32)
    low = base - prod.reshape(-1, tile, tile)
    at_lo = my_row == n_row - 2
    s_row = jnp.where(at_lo, s[:tile], s[tile:])
    t_row = jnp.where(at_lo, t[:tile], t[tile:])
    own = fresh - (t_row + dot3(s_row, l_dk.astype(F32)))
    d_row = jnp.where(at_lo, out_dd[:tile], out_dd[tile:])
    d_own = jnp.where(my_col == lo, d_row[:, :tile], d_row[:, tile:])
    in_panel = my_row >= n_row - 2
    zt = jnp.zeros_like(fresh)
    own = jnp.where(in_panel, jnp.where(right, d_own, own), jnp.where(right, zt, fresh))
    upper = jnp.where(right, jnp.zeros((), BF16), grad[:loc]).astype(F32)
    out = jnp.concatenate([upper, own[None], low], 0)
    return out.reshape(l_grad.shape)


def solution(mesh):
    spec = P(None, "row", None, "col", None)
    return jax.shard_map(
        per_device, mesh=mesh, in_specs=(spec, spec), out_specs=spec, check_vma=False
    )
```

profile of v0, /device:TPU:0, one launch (start us, length us, event | category | flops | bytes accessed | tf_op | source)
XLA Modules:
  0.0 323.6 jit_solution(8879946724786427271)
XLA Ops:
  6.5 0.9 slice.87
  7.5 8.7 %all-gather = bf16[4,1,256,1,256]{4,2,3,1,0:T(8,128)(2,1)S(1)} all-gather(bf16[1,1,256,1,256]{4,2,3,1,0:T(8,128)(2,1)S(1)} %slice.87), channel_id=2, replica_groups=mesh['row'=4,'col'=8] {'row'}, dimensions={0}, use_global_device_ids=true | all-gather | bytes 655360 | tf_op jit(solution)/shard_map/all_gather | solution.py:54
  16.2 1.7 slice.115
  17.9 0.7 broadcast_select_fusion.1
  18.6 2.3 pad_maximum_fusion
  21.0 1.5 copy-done.3
  22.5 0.7 bitcast_convert_fusion
  23.2 7.3 %all-gather.1 = bf16[4,1,256,1,256]{4,2,3,1,0:T(8,128)(2,1)S(1)} all-gather(bf16[1,1,256,1,256]{4,2,3,1,0:T(8,128)(2,1)S(1)} %get-tuple-element.8), channel_id=3, replica_groups=mesh['row'=4,'col'=8] {'row'}, dimensions={0}, use_global_device_ids=true | all-gather | bytes 655360 | tf_op jit(solution)/shard_map/all_gather | solution.py:73
  30.5 0.7 slice.122
  31.5 0.2 fusion.85
  32.9 145.4 %all-reduce.5.cloned.1.call-done = bf16[4096,512]{1,0:T(8,128)(2,1)} async-done(((bf16[4096,512]{1,0:T(8,128)(2,1)}), bf16[4096,512]{1,0:T(8,128)(2,1)}) %all-reduce.5.cloned.1.call-update) | async-done | bytes 4194320 | tf_op jit(solution)/shard_map/psum | solution.py:60
  178.3 1.2 slice_convert_fusion
  179.7 0.5 fusion.34
  180.2 0.5 convolution_subtract_fusion.6
  180.7 0.4 fusion.32
  181.1 0.4 convolution_subtract_fusion.5
  181.5 0.4 fusion.30
  181.9 0.4 convolution_subtract_fusion.4
  182.3 0.4 fusion.28
  182.7 0.4 convolution_subtract_fusion.3
  183.1 0.4 fusion.26
  183.5 0.4 convolution_subtract_fusion.2
  183.9 0.4 fusion.24
  184.3 0.4 convolution_subtract_fusion.1
  184.7 0.4 fusion.22
  185.2 0.4 convolution_subtract_fusion
  185.6 0.5 copy-done
  186.1 0.2 fusion.99
  186.4 0.3 convolution_negate_fusion
  186.8 1.9 fusion.3
  188.8 0.2 all-reduce.9.cloned.1.call-start
  189.1 1.4 convolution_select_fusion
  190.5 30.8 %all-reduce.7.cloned.1.call-done = f32[512,256]{1,0:T(8,128)} async-done(((f32[512,256]{1,0:T(8,128)}), f32[512,256]{1,0:T(8,128)}) %all-reduce.7.cloned.1.call-update) | async-done | bytes 524304 | tf_op jit(solution)/shard_map/psum | solution.py:71
  221.3 2.7 fusion.40
  224.0 1.2 pad_maximum_fusion.3
  225.2 3.3 %fusion.1 = f32[3584,256]{1,0:T(8,128)S(1)} fusion(bf16[4096,512]{1,0:T(8,128)(2,1)} %all-reduce.5.cloned.1.call-done, f32[512,256]{1,0:T(8,128)S(1)} %convolution_select_fusion), kind=kOutput, calls=%fused_computation.5 | convolution fusion | flops 939786240 | bytes 7864320 | tf_op jit(solution)/shard_map/dot_general | solution.py:95
  228.5 1.1 convolution_add_fusion
  229.7 2.3 convert_subtract_fusion
  231.9 71.8 %all-reduce.9.cloned.1.call-done = f32[512,512]{1,0:T(8,128)} async-done(((f32[512,512]{1,0:T(8,128)}), f32[512,512]{1,0:T(8,128)}) %all-reduce.9.cloned.1.call-update) | async-done | bytes 1048592 | tf_op jit(solution)/shard_map/psum | solution.py:76
  303.7 2.2 fusion.14
  305.9 1.0 fusion.9
  307.0 2.0 fusion.113
  309.0 1.3 copy.12
  310.3 1.6 select_subtract_fusion
  312.1 0.3 fusion.8
  312.4 0.5 copy-done.2
  312.8 0.4 pad_maximum_fusion.1
  313.2 3.9 %reshape.79 = f32[16,1,256,1,256]{4,3,2,1,0:T(1,128)} reshape(f32[16,256,256]{2,1,0:T(8,128)S(1)} %pad_maximum_fusion.1) | data formatting | bytes 8388608 | tf_op jit(solution)/shard_map/reshape | solution.py:111
  (53 shorter events, 2.0 us)
Async XLA Ops:
  6.5 171.8 %all-reduce.5.cloned.1.call-start = ((), (), s32[]{:S(2)}) async-start(), calls=%async_computation | async-start | bytes 8388608 | tf_op jit(solution)/shard_map/psum | solution.py:60
  16.2 2.4 copy-start.6
  20.9 1.6 copy-start.3
  20.9 200.4 %all-reduce.7.cloned.1.call-start = ((), (), s32[]{:S(2)}) async-start(), calls=%async_computation.1 | async-start | bytes 1048576 | tf_op jit(solution)/shard_map/psum | solution.py:71
  183.9 2.2 copy-start
  184.3 2.5 slice-start
  186.1 119.8 %copy-start.4 = (f32[256,256]{1,0:T(8,128)}, f32[256,256]{1,0:T(8,128)S(1)}, u32[]{:S(2)}) copy-start(f32[256,256]{1,0:T(8,128)S(1)} %get-tuple-element.15) | copy-start | bytes 786436
  186.1 119.8 %copy-start.5 = (f32[256,256]{1,0:T(8,128)}, f32[256,256]{1,0:T(8,128)S(1)}, u32[]{:S(2)}) copy-start(f32[256,256]{1,0:T(8,128)S(1)} %get-tuple-element.16) | copy-start | bytes 786436
  188.8 115.0 %all-reduce.9.cloned.1.call-start = ((), (), s32[]{:S(2)}) async-start(), calls=%async_computation.2 | async-start | bytes 2097152 | tf_op jit(solution)/shard_map/psum | solution.py:76
  225.2 3.3 %copy-start.1 = (bf16[4096,512]{1,0:T(8,128)(2,1)S(1)}, bf16[4096,512]{1,0:T(8,128)(2,1)}, u32[]{:S(2)}) copy-start(bf16[4096,512]{1,0:T(8,128)(2,1)} %all-reduce.5.cloned.1.call-done) | copy-start | bytes 12582916
  309.0 3.1 copy-start.7
  310.3 1.7 copy-start.9
  310.3 2.5 copy-start.2
  310.3 2.5 copy-start.8
Sparse Core Ops, SparseCore 0:
  21.1 157.1 all-reduce.4
  188.9 32.3 all-reduce.6
  225.3 78.3 all-reduce.8
where the time goes:
time: 324 us
  waiting for transfers between devices  248 us (77%)
  matrix products  22.3 us (7%)
  blocking collectives  15.9 us (5%)
  between operations  13.6 us (4%)
  other arithmetic  12.1 us (4%)
  local copies, waits for them, and re-layouts  11.3 us (3%)
    psum x1, waiting for transfers between devices, per_device(): both = lax.psum(both, 'col')  145 us
    psum x1, waiting for transfers between devices, per_device(): lax.psum(jnp.concatenate([jnp.where(my_col == lo, q_mine, z2), jnp.where(...  71.8 us
    psum x1, waiting for transfers between devices, per_device(): t = dot3(w, lax.psum(h, 'row'), 0, 0)  30.8 us
    dot_general x8, matrix products, dot3(): lax.dot_general(a, b, (((ca,), (cb,)), ((), ())), precision=HIGH3, prefer...  10.1 us
    all_gather x1, blocking collectives, per_device(): lax.all_gather(factor[loc], 'row')[n_row - 2:].reshape(2 * tile, tile)  8.68 us
    all_gather x1, blocking collectives, per_device(): lax.all_gather(grad[loc], 'row')[n_row - 2:].reshape(2 * tile, tile)  7.26 us
  transfers between devices with their start and end apart: 3, of which 3 were waited for; matrix products, arithmetic and copies ran while one was open for 3% of the time, Pallas kernels for 0%

commit v1 on v0

--- a/solution.py
+++ b/solution.py
@@ -57,7 +57,9 @@
     both = jnp.concatenate(
         [jnp.where(my_col == lo, mine, zero), jnp.where(my_col == hi, mine, zero)], 1
     )
-    both = lax.psum(both, "col")
+    both = both
+    for hop in (1, 2, 4):
+        both = both + lax.ppermute(both, "col", [(dev, dev ^ hop) for dev in range(8)])
     l_dd = both[: 2 * tile].astype(F32)
     g_d = both[2 * tile :]
     l66, l76, l77 = (l_dd[:tile, :tile], l_dd[tile:, :tile], l_dd[tile:, tile:])

time: 324 us -> 541 us (1.67)
  waiting for transfers between devices: 248 us -> 456 us
  other arithmetic: 12.1 us -> 18.2 us
  starting transfers between devices: 0.27 us -> 6.05 us
    ppermute x0 -> x3, waiting for transfers between devices: none -> 351 us  [per_device(): lax.ppermute(both, 'col', [(dev, dev ^ hop) for dev in range(8)])]
    psum x1 -> x0, waiting for transfers between devices: 145 us -> none  [per_device(): both = lax.psum(both, 'col')]
    add x0 -> x3, other arithmetic: none -> 9.18 us  [per_device(): both + lax.ppermute(both, 'col', [(dev, dev ^ hop) for dev in range(8)])]
    ppermute x0 -> x3, starting transfers between devices: none -> 5.79 us  [per_device(): lax.ppermute(both, 'col', [(dev, dev ^ hop) for dev in range(8)])]
  transfers between devices with their start and end apart: 3 -> 5, of which waited for: 3 -> 5; matrix products, arithmetic and copies ran while one was open for 3% -> 2% of each run, Pallas kernels for 0% -> 0%
where the time goes in v1:
time: 541 us
  waiting for transfers between devices  456 us (84%)
  matrix products  22.3 us (4%)
  other arithmetic  18.2 us (3%)
  blocking collectives  15.6 us (3%)
  between operations  13.9 us (3%)
  local copies, waits for them, and re-layouts  9.13 us (2%)
  starting transfers between devices  6.05 us (1%)
    ppermute x3, waiting for transfers between devices, per_device(): lax.ppermute(both, 'col', [(dev, dev ^ hop) for dev in range(8)])  351 us
    psum x1, waiting for transfers between devices, per_device(): lax.psum(jnp.concatenate([jnp.where(my_col == lo, q_mine, z2), jnp.where(...  71.8 us
    psum x1, waiting for transfers between devices, per_device(): t = dot3(w, lax.psum(h, 'row'), 0, 0)  32.4 us
  transfers between devices with their start and end apart: 5, of which 5 were waited for; matrix products, arithmetic and copies ran while one was open for 2% of the time, Pallas kernels for 0%

profile of v1, /device:TPU:0, one launch (start us, length us, event | category | flops | bytes accessed | tf_op | source)
XLA Modules:
  0.0 540.9 jit_solution(16961997449021672686)
XLA Ops:
  6.5 0.9 slice.87
  7.5 8.7 %all-gather = bf16[4,1,256,1,256]{4,2,3,1,0:T(8,128)(2,1)S(1)} all-gather(bf16[1,1,256,1,256]{4,2,3,1,0:T(8,128)(2,1)S(1)} %slice.87), channel_id=2, replica_groups=mesh['row'=4,'col'=8] {'row'}, dimensions={0}, use_global_device_ids=true | all-gather | bytes 655360 | tf_op jit(solution)/shard_map/all_gather | solution.py:54
  16.2 1.7 slice.115
  17.9 0.7 broadcast_select_fusion.1
  18.9 1.6 collective-permute-start
  20.5 91.3 %collective-permute-done = bf16[4096,512]{1,0:T(8,128)(2,1)S(1)} collective-permute-done((bf16[4096,512]{1,0:T(8,128)(2,1)S(1)}, bf16[4096,512]{1,0:T(8,128)(2,1)S(1)}, u32[]{:S(2)}, u32[]{:S(2)}) %collective-permute-start) | collective-permute-done | bytes 4194336 | tf_op jit(solution)/shard_map/ppermute | solution.py:62
  111.8 1.1 fusion.115
  112.9 1.6 collective-permute-start.1
  114.6 90.4 %collective-permute-done.1 = bf16[4096,512]{1,0:T(8,128)(2,1)S(1)} collective-permute-done((bf16[4096,512]{1,0:T(8,128)(2,1)S(1)}, bf16[4096,512]{1,0:T(8,128)(2,1)S(1)}, u32[]{:S(2)}, u32[]{:S(2)}) %collective-permute-start.1) | collective-permute-done | bytes 4194336 | tf_op jit(solution)/shard_map/ppermute | solution.py:62
  205.0 3.4 add.99
  208.4 2.6 collective-permute-start.2
  211.0 0.7 bitcast_convert_fusion
  211.7 6.9 %all-gather.1 = bf16[4,1,256,1,256]{4,2,3,1,0:T(8,128)(2,1)S(1)} all-gather(bf16[1,1,256,1,256]{4,2,3,1,0:T(8,128)(2,1)S(1)} %get-tuple-element.8), channel_id=3, replica_groups=mesh['row'=4,'col'=8] {'row'}, dimensions={0}, use_global_device_ids=true | all-gather | bytes 655360 | tf_op jit(solution)/shard_map/all_gather | solution.py:75
  218.6 0.7 slice.122
  221.0 169.6 %collective-permute-done.2 = bf16[4096,512]{1,0:T(8,128)(2,1)} collective-permute-done((bf16[4096,512]{1,0:T(8,128)(2,1)}, bf16[4096,512]{1,0:T(8,128)(2,1)}, u32[]{:S(2)}, u32[]{:S(2)}) %collective-permute-start.2) | collective-permute-done | bytes 4194336 | tf_op jit(solution)/shard_map/ppermute | solution.py:62
  390.6 4.7 add.100
  395.6 0.5 fusion.34
  396.2 0.5 convolution_subtract_fusion.6
  396.7 0.4 fusion.32
  397.1 0.4 convolution_subtract_fusion.5
  397.5 0.4 fusion.30
  397.9 0.4 convolution_subtract_fusion.4
  398.3 0.4 fusion.28
  398.7 0.4 convolution_subtract_fusion.3
  399.1 0.4 fusion.26
  399.5 0.4 convolution_subtract_fusion.2
  399.9 0.4 fusion.24
  400.3 0.4 convolution_subtract_fusion.1
  400.7 0.4 fusion.22
  401.1 0.4 convolution_subtract_fusion
  402.1 2.0 fusion.3
  404.5 1.4 convolution_select_fusion
  405.9 32.4 %all-reduce.4.cloned.1.call-done = f32[512,256]{1,0:T(8,128)} async-done(((f32[512,256]{1,0:T(8,128)}), f32[512,256]{1,0:T(8,128)}) %all-reduce.4.cloned.1.call-update) | async-done | bytes 524304 | tf_op jit(solution)/shard_map/psum | solution.py:73
  438.3 2.7 fusion.40
  441.1 1.1 pad_maximum_fusion.3
  442.2 3.3 fusion
  445.6 1.1 convolution_add_fusion
  446.7 2.2 convert_subtract_fusion
  448.9 71.8 %all-reduce.6.cloned.1.call-done = f32[512,512]{1,0:T(8,128)} async-done(((f32[512,512]{1,0:T(8,128)}), f32[512,512]{1,0:T(8,128)}) %all-reduce.6.cloned.1.call-update) | async-done | bytes 1048592 | tf_op jit(solution)/shard_map/psum | solution.py:78
  520.7 2.2 fusion.14
  522.9 1.0 fusion.9
  523.9 2.0 fusion.113
  525.9 1.3 copy.12
  527.2 1.6 select_subtract_fusion
  529.0 0.3 fusion.8
  529.3 0.4 copy-done.2
  529.8 0.4 pad_maximum_fusion.1
  530.2 3.9 reshape.79
  (58 shorter events, 3.2 us)
Async XLA Ops:
  6.5 431.8 %all-reduce.4.cloned.1.call-start = ((), (), s32[]{:S(2)}) async-start(), calls=%async_computation | async-start | bytes 1048576 | tf_op jit(solution)/shard_map/psum | solution.py:73
  16.2 2.4 copy-start.6
  18.9 92.9 %collective-permute-start = (bf16[4096,512]{1,0:T(8,128)(2,1)S(1)}, bf16[4096,512]{1,0:T(8,128)(2,1)S(1)}, u32[]{:S(2)}, u32[]{:S(2)}) collective-permute-start(bf16[4096,512]{1,0:T(8,128)(2,1)S(1)} %pad_maximum_fusion), channel_id=1, source_target_pairs={{0,1},{1,0},{2,3},{3,2},{4,5},{5,4},{6,7},{7,6},{8,9},{9,8},{10,11... | collective-permute-start | bytes 12582920 | tf_op jit(solution)/shard_map/ppermute | solution.py:62
  112.9 98.0 %copy-start.3 = (bf16[16,1,256,1,256]{4,2,3,1,0:T(8,128)(2,1)S(1)}, bf16[16,1,256,1,256]{4,2,3,1,0:T(8,128)(2,1)}, u32[]{:S(2)}) copy-start(bf16[16,1,256,1,256]{4,2,3,1,0:T(8,128)(2,1)} %param.3) | copy-start | bytes 6291460
  112.9 92.0 %collective-permute-start.1 = (bf16[4096,512]{1,0:T(8,128)(2,1)S(1)}, bf16[4096,512]{1,0:T(8,128)(2,1)S(1)}, u32[]{:S(2)}, u32[]{:S(2)}) collective-permute-start(bf16[4096,512]{1,0:T(8,128)(2,1)S(1)} %fusion.115), channel_id=1, source_target_pairs={{0,2},{1,3},{2,0},{3,1},{4,6},{5,7},{6,4},{7,5},{8,10},{9,11},{10,... | collective-permute-start | bytes 12582920 | tf_op jit(solution)/shard_map/ppermute | solution.py:62
  208.4 182.2 %collective-permute-start.2 = (bf16[4096,512]{1,0:T(8,128)(2,1)}, bf16[4096,512]{1,0:T(8,128)(2,1)}, u32[]{:S(2)}, u32[]{:S(2)}) collective-permute-start(bf16[4096,512]{1,0:T(8,128)(2,1)} %add.99), channel_id=1, source_target_pairs={{0,4},{1,5},{2,6},{3,7},{4,0},{5,1},{6,2},{7,3},{8,12},{9,13},{10,... | collective-permute-start | bytes 12582920 | tf_op jit(solution)/shard_map/ppermute | solution.py:62
  395.2 6.9 %copy-start = (bf16[4096,512]{1,0:T(8,128)(2,1)}, bf16[4096,512]{1,0:T(8,128)(2,1)S(1)}, u32[]{:S(2)}) copy-start(bf16[4096,512]{1,0:T(8,128)(2,1)S(1)} %add.100) | copy-start | bytes 12582916
  399.9 2.2 slice-start
  401.8 121.0 %copy-start.4 = (f32[256,256]{1,0:T(8,128)}, f32[256,256]{1,0:T(8,128)S(1)}, u32[]{:S(2)}) copy-start(f32[256,256]{1,0:T(8,128)S(1)} %get-tuple-element.15) | copy-start | bytes 786436
  401.8 121.0 %copy-start.5 = (f32[256,256]{1,0:T(8,128)}, f32[256,256]{1,0:T(8,128)S(1)}, u32[]{:S(2)}) copy-start(f32[256,256]{1,0:T(8,128)S(1)} %get-tuple-element.16) | copy-start | bytes 786436
  404.1 116.6 %all-reduce.6.cloned.1.call-start = ((), (), s32[]{:S(2)}) async-start(), calls=%async_computation.1 | async-start | bytes 2097152 | tf_op jit(solution)/shard_map/psum | solution.py:78
  442.2 3.3 copy-start.1
  525.9 3.0 copy-start.7
  527.2 1.7 copy-start.9
  527.2 2.5 copy-start.2
  527.2 2.5 copy-start.8
Sparse Core Ops, SparseCore 0:
  404.2 34.0 all-reduce.3
  442.4 78.2 all-reduce.5
